TPU v7x, 32 devices: a whole 2x2x4 slice. The times are simulated.
32 devices in a mesh: gx: 4 (over z), gy: 8 (over y, x, core).
Axes of the slice: x: 2, y: 2, z: 4, core: 2. Of those that a mesh axis runs over, the one named last changes fastest.
Arguments:
- tokens: bfloat16 [28672, 4096], P(('gx', 'gy')), may hold values from -6 to 6
- codes: bfloat16 [4096, 512], P(('gx', 'gy')), may hold values from -0.09375 to 0.09375
- scales: float32 [128, 4], P(('gx', 'gy')), may hold values from 0.5 to 2
- gain: float32 [128], replicated, may hold values from 0.1 to 1.9
- cotangent: bfloat16 [28672, 512], P(('gx', 'gy')), may hold values from -96 to 96
Outputs:
- keys: bfloat16 [28672, 512], P(('gx', 'gy'))
- token_grad: bfloat16 [28672, 4096], P(('gx', 'gy'))
- weight_grad: float32 [4096, 512], P(('gx', 'gy'))
All inputs are finite; a program needn't handle non-finite values.
Results may differ from a plain program's by a relative error of at most 0.019.
Values may be sent and summed in bfloat16 or wider, within the bound.
No kernel may reach another device: no remote copies, remote signals or barrier semaphores. Data moves between devices by JAX's collectives and lax.ppermute only.
A program may use at most 128 MiB of HBM per device.

v0:
```python
import math
import jax
import jax.numpy as jnp
from jax import lax
from jax.sharding import PartitionSpec as P

KV_HEADS = 4
HEAD = 128
QBLK = 32
clip_ratio = 2.5


def hadamard(length):
    indices = jnp.arange(length, dtype=jnp.int32)
    common = jnp.bitwise_and(indices[:, None], indices[None, :])
    parity = jnp.zeros((length, length), jnp.int32)
    for position in range(length.bit_length() - 1):
        parity = parity + jnp.bitwise_and(jnp.right_shift(common, position), 1)
    return (1 - 2 * (parity % 2)).astype(jnp.float32) / math.sqrt(length)


def rotate(matrix, rotation):
    shaped = matrix.reshape(matrix.shape[0], KV_HEADS, HEAD)
    rotated = jnp.einsum("rhc,cd->rhd", shaped, rotation, precision=lax.Precision.HIGHEST)
    return rotated.reshape(matrix.shape)


def clipped(matrix):
    shaped = matrix.reshape(matrix.shape[0] // QBLK, QBLK, KV_HEADS, HEAD)
    mean_square = jnp.mean(shaped * shaped, axis=(1, 3), keepdims=True)
    clip_bound = clip_ratio * jnp.sqrt(mean_square + 1e-06)
    return jnp.clip(shaped, -clip_bound, clip_bound).reshape(matrix.shape)


def normed_keys(projected, gain):
    shaped = projected.reshape(projected.shape[0], KV_HEADS, HEAD)
    mean_square = jnp.mean(shaped * shaped, axis=-1, keepdims=True)
    return (shaped * lax.rsqrt(mean_square + 1e-06) * gain).reshape(projected.shape)


def scaled(values, block_scales):
    block_count = block_scales.shape[0]
    blocks = values.astype(jnp.float32).reshape(
        block_count, values.shape[0] // block_count, KV_HEADS, HEAD
    )
    return (blocks * block_scales[:, None, :, None]).reshape(values.shape).astype(jnp.bfloat16)


def collect(pieces):
    outer_count = lax.axis_size("gx")
    inner_count = lax.axis_size("gy")
    near_rows = lax.all_gather(pieces, "gx", axis=0, tiled=True)
    gathered = lax.all_gather(near_rows, "gy", axis=0, tiled=True)
    shaped = gathered.reshape(
        (inner_count, outer_count, gathered.shape[0] // (inner_count * outer_count))
        + gathered.shape[1:]
    )
    return jnp.swapaxes(shaped, 0, 1).reshape(gathered.shape)


def body(tokens, codes, scales, gain, cotangent):
    weight = collect(scaled(codes, scales))
    projected = jnp.dot(tokens, weight, preferred_element_type=jnp.float32)
    normed, pullback = jax.vjp(lambda value_in: normed_keys(value_in, gain), projected)
    keys_out = normed.astype(jnp.bfloat16)
    key_grad = pullback(cotangent.astype(jnp.float32))[0].astype(jnp.bfloat16)
    token_grad = lax.dot_general(
        key_grad, weight, (((1,), (1,)), ((), ())), preferred_element_type=jnp.float32
    ).astype(jnp.bfloat16)
    rotation = hadamard(HEAD)
    partial_value = lax.dot_general(
        tokens, key_grad, (((0,), (0,)), ((), ())), preferred_element_type=jnp.float32
    )
    level_one = lax.psum_scatter(
        clipped(rotate(partial_value, rotation)).astype(jnp.bfloat16),
        "gx",
        scatter_dimension=0,
        tiled=True,
    ).astype(jnp.float32)
    recoded = clipped(level_one)
    level_two = lax.psum_scatter(
        recoded.astype(jnp.bfloat16), "gy", scatter_dimension=0, tiled=True
    ).astype(jnp.float32)
    weight_grad = rotate(level_two, rotation)
    return (keys_out, token_grad, weight_grad)


def solution(mesh):
    in_specs = (
        P(("gx", "gy"), None),
        P(("gx", "gy"), None),
        P(("gx", "gy"), None),
        P(),
        P(("gx", "gy"), None),
    )
    out_specs = (P(("gx", "gy"), None), P(("gx", "gy"), None), P(("gx", "gy"), None))
    return jax.shard_map(body, mesh=mesh, in_specs=in_specs, out_specs=out_specs, check_vma=False)
```

profile of v0, /device:TPU:0, one launch (start us, length us, event | category | flops | bytes accessed | tf_op | source)
XLA Modules:
  0.0 265.3 jit_solution(8661850951664697459)
XLA Ops:
  7.2 0.0 all-gather.2.cloned.1.call-start
  7.2 0.8 mul.121
  8.0 0.9 fusion.7
  8.9 18.0 %all_gather.6 = bf16[512,512]{1,0:T(8,128)(2,1)} all-gather(bf16[128,512]{1,0:T(8,128)(2,1)S(1)} %fusion.7), channel_id=1, replica_groups=mesh['gx'=4,'gy'=8] {'gx'}, dimensions={0}, use_global_device_ids=true | all-gather | bytes 655360 | tf_op jit(solution)/shard_map/all_gather | solution.py:52
  26.9 0.0 all-gather.2.cloned.1.call-update
  27.0 0.0 reduce-scatter.3.cloned.1.call-start
  27.0 1.5 copy.21
  28.6 0.7 broadcast_bitcast_fusion
  29.2 36.4 %all-gather.2.cloned.1.call-done = bf16[4096,512]{1,0:T(8,128)(2,1)} async-done(((bf16[512,512]{1,0:T(8,128)(2,1)}), bf16[4096,512]{1,0:T(8,128)(2,1)}) %all-gather.2.cloned.1.call-update) | async-done | bytes 4194320 | tf_op jit(solution)/shard_map/all_gather | solution.py:53
  65.6 0.0 copy-start.1
  65.6 0.0 copy-start.6
  65.6 2.7 %copy.20 = bf16[4,8,128,512]{3,2,1,0:T(8,128)(2,1)S(1)} copy(bf16[4,8,128,512]{3,2,0,1:T(8,128)(2,1)} %bitcast.72) | data formatting | bytes 8388608 | tf_op jit(solution)/shard_map/transpose | solution.py:58
  68.3 0.0 copy-start
  68.3 3.2 %copy-done.1 = bf16[896,4096]{1,0:T(8,128)(2,1)S(1)} copy-done((bf16[896,4096]{1,0:T(8,128)(2,1)S(1)}, bf16[896,4096]{1,0:T(8,128)(2,1)}, u32[]{:S(2)}) %copy-start.1) | copy-done | bytes 7340056
  71.4 0.0 copy-done.6
  71.4 4.7 %multiply_reduce_fusion.1 = (f32[896,4]{0,1:T(4,128)S(1)}, f32[896,4]{0,1:T(4,128)S(1)}, f32[512,896]{1,0:T(8,128)S(1)}) fusion(f32[128]{0:T(128)S(1)} %copy-done.6, bf16[896,512]{0,1:T(8,128)(2,1)S(1)} %copy.21, bf16[4096,512]{1,0:T(8,128)(2,1)S(1)} %bitcast.70, bf16[896,4096]{1,0:T(8,128)(2,1)S(1)} %copy-done.1), kind=kOutput, calls=%fused_computation.18 | convolution fusion | flops 3760841728 | bytes 14316032 | tf_op jit(solution)/shard_map/dot_general | solution.py:63
  76.2 0.0 copy-done
  76.2 1.5 fusion.4
  77.7 0.0 copy-start.4
  77.7 0.9 copy-done.4
  78.7 6.7 %convolution_bitcast_fusion = f32[4096,512]{0,1:T(8,128)} fusion(bf16[896,512]{0,1:T(8,128)(2,1)S(1)} %get-tuple-element.14, bf16[896,4096]{1,0:T(8,128)(2,1)S(1)} %copy-done.1), kind=kOutput, calls=%fused_computation.5 | convolution fusion | flops 3758096384 | bytes 16646144 | tf_op jit(solution)/shard_map/dot_general | solution.py:71
  85.3 9.0 %copy.22 = f32[4096,512]{1,0:T(8,128)} copy(f32[4096,512]{0,1:T(8,128)} %convolution_bitcast_fusion) | data formatting | bytes 16777216 | tf_op jit(solution)/shard_map/dot_general | solution.py:71
  94.3 9.9 %dot_general.26 = f32[128,32,4,128]{3,2,1,0:T(4,128)} reshape(f32[4096,512]{1,0:T(8,128)} %copy.22) | data formatting | bytes 16777216 | tf_op jit(solution)/shard_map/rhc,cd->rhd/dot_general | solution.py:24
  104.2 16.1 %multiply_reduce_fusion = (f32[128,4]{0,1:T(4,128)S(1)}, bf16[128,32,4,128]{0,3,2,1:T(8,128)(2,1)S(1)}) fusion(f32[128,32,4,128]{3,2,1,0:T(4,128)} %dot_general.26), kind=kOutput, calls=%fused_computation.3 | convolution fusion | flops 3228106240 | bytes 12584960 | tf_op jit(solution)/shard_map/rhc,cd->rhd/dot_general | solution.py:24
  120.4 2.3 minimum_convert_fusion
  122.7 7.9 %copy.24 = bf16[128,32,4,128]{3,2,1,0:T(4,128)(2,1)} copy(bf16[128,32,4,128]{0,3,2,1:T(8,128)(2,1)} %minimum_convert_fusion) | data formatting | bytes 8388608 | tf_op jit(solution)/shard_map/convert_element_type | solution.py:75
  130.7 4.9 %copy.43 = bf16[512,8,4,128]{3,1,2,0:T(8,128)(2,1)} copy(bf16[512,8,4,128]{3,2,1,0:T(4,128)(2,1)} %bitcast.69) | data formatting | bytes 8388608
  135.6 0.0 reduce-scatter.3.cloned.1.call-update
  135.6 0.0 reduce-scatter.5.cloned.1.call-start
  135.7 76.9 %reduce-scatter.3.cloned.1.call-done = bf16[1024,512]{1,0:T(8,128)(2,1)} async-done(((bf16[4096,512]{1,0:T(8,128)(2,1)}), bf16[1024,512]{1,0:T(8,128)(2,1)}) %reduce-scatter.3.cloned.1.call-update) | async-done | bytes 1048592 | tf_op jit(solution)/shard_map/reduce_scatter | solution.py:74
  212.6 2.8 %convert_multiply_fusion = f32[1024,512]{1,0:T(8,128)} fusion(bf16[1024,512]{1,0:T(8,128)(2,1)} %reduce-scatter.3.cloned.1.call-done), kind=kLoop, calls=%fused_computation.11 | loop fusion | flops 1048576 | bytes 3145728 | tf_op jit(solution)/shard_map/mul | solution.py:30
  215.4 0.0 copy-start.2
  215.4 2.0 mul.146
  217.4 0.4 reduce_sum.43
  217.8 0.0 copy-start.3
  217.8 0.3 min.29
  218.2 0.0 copy-start.5
  218.2 0.3 max.29
  218.5 0.0 copy-done.2
  218.5 1.4 fusion.3
  220.0 0.0 reduce-scatter.5.cloned.1.call-update
  220.0 0.0 copy-done.3
  220.0 1.3 copy.27
  221.3 0.0 copy-done.5
  221.3 9.3 %convolution_convert_fusion = bf16[896,4096]{1,0:T(8,128)(2,1)} fusion(bf16[896,512]{0,1:T(8,128)(2,1)S(1)} %copy-done.5, bf16[4096,512]{1,0:T(8,128)(2,1)} %bitcast.71), kind=kOutput, calls=%fused_computation.4 | convolution fusion | flops 3761766400 | bytes 12451840 | tf_op jit(solution)/shard_map/dot_general | solution.py:67
  230.6 26.0 %reduce-scatter.5.cloned.1.call-done = bf16[128,512]{1,0:T(8,128)(2,1)} async-done(((bf16[1024,512]{1,0:T(8,128)(2,1)}), bf16[128,512]{1,0:T(8,128)(2,1)}) %reduce-scatter.5.cloned.1.call-update) | async-done | bytes 131088 | tf_op jit(solution)/shard_map/reduce_scatter | solution.py:81
  256.6 1.0 copy.25
  257.6 0.3 fusion.14
  258.0 0.8 copy.28
  (3 shorter events, 0.0 us)
Async XLA Ops:
  7.2 58.4 %all-gather.2.cloned.1.call-start = ((), (), s32[]{:S(2)}) async-start(), calls=%async_computation.2 | async-start | bytes 4718592 | tf_op jit(solution)/shard_map/all_gather | solution.py:53
  27.0 185.6 %reduce-scatter.3.cloned.1.call-start = ((), (), s32[]{:S(2)}) async-start(), calls=%async_computation.3 | async-start | bytes 5242880 | tf_op jit(solution)/shard_map/reduce_scatter | solution.py:74
  65.6 5.9 %copy-start.1 = (bf16[896,4096]{1,0:T(8,128)(2,1)S(1)}, bf16[896,4096]{1,0:T(8,128)(2,1)}, u32[]{:S(2)}) copy-start(bf16[896,4096]{1,0:T(8,128)(2,1)} %param.5) | copy-start | bytes 22020100
  65.6 5.9 %copy-start.6 = (f32[128]{0:T(128)S(1)}, f32[128]{0:T(128)}, u32[]{:S(2)}) copy-start(f32[128]{0:T(128)} %param.8) | copy-start | bytes 1540
  68.3 7.9 %copy-start = (bf16[4,8,128,512]{3,2,1,0:T(8,128)(2,1)}, bf16[4,8,128,512]{3,2,1,0:T(8,128)(2,1)S(1)}, u32[]{:S(2)}) copy-start(bf16[4,8,128,512]{3,2,1,0:T(8,128)(2,1)S(1)} %copy.20) | copy-start | bytes 12582916
  77.7 0.9 copy-start.4
  135.6 121.0 %reduce-scatter.5.cloned.1.call-start = ((), (), s32[]{:S(2)}) async-start(), calls=%async_computation.4 | async-start | bytes 1179648 | tf_op jit(solution)/shard_map/reduce_scatter | solution.py:81
  215.4 3.1 %copy-start.2 = (bf16[1024,512]{1,0:T(8,128)(2,1)S(1)}, bf16[1024,512]{1,0:T(8,128)(2,1)}, u32[]{:S(2)}) copy-start(bf16[1024,512]{1,0:T(8,128)(2,1)} %reduce-scatter.3.cloned.1.call-done) | copy-start | bytes 3145732
  217.8 2.2 copy-start.3
  218.2 3.1 %copy-start.5 = (bf16[896,512]{0,1:T(8,128)(2,1)S(1)}, bf16[896,512]{0,1:T(8,128)(2,1)}, u32[]{:S(2)}) copy-start(bf16[896,512]{0,1:T(8,128)(2,1)} %copy-done.4) | copy-start | bytes 2752516
Sparse Core Ops, SparseCore 0:
  27.1 38.4 all-gather.1
  135.7 76.7 reduce-scatter.2
  220.1 36.4 reduce-scatter.4
where the time goes:
time: 266 us; the launch traced here: 265 us
  waiting for transfers between devices  139 us (52%)
  local copies, waits for them, and re-layouts  47.4 us (18%)
  matrix products  37.1 us (14%)
  blocking collectives  18 us (7%)
  between operations  13.9 us (5%)
  other arithmetic  9.49 us (4%)
    reduce_scatter x1, waiting for transfers between devices, body(): lax.psum_scatter(clipped(rotate(partial_value, rotation)).astype(jnp.bflo...  76.9 us
    all_gather x1, waiting for transfers between devices, collect(): gathered = lax.all_gather(near_rows, 'gy', axis=0, tiled=True)  36.4 us
    reduce_scatter x1, waiting for transfers between devices, body(): lax.psum_scatter(recoded.astype(jnp.bfloat16), 'gy', scatter_dimension=0,...  26 us
    all_gather x1, blocking collectives, collect(): near_rows = lax.all_gather(pieces, 'gx', axis=0, tiled=True)  18 us
    dot_general x2, matrix products, rotate(): jnp.einsum('rhc,cd->rhd', shaped, rotation, precision=lax.Precision.HIGHEST)  16.4 us
    unnamed x18, local copies, waits for them, and re-layouts  12.7 us
    dot_general x1, local copies, waits for them, and re-layouts, rotate(): jnp.einsum('rhc,cd->rhd', shaped, rotation, precision=lax.Precision.HIGHEST)  9.9 us
    dot_general x1, matrix products, body(): lax.dot_general(key_grad, weight, (((1,), (1,)), ((), ())), preferred_ele...  9.27 us
  transfers between devices with their start and end apart: 3, of which 3 were waited for; matrix products, arithmetic and copies ran while one was open for 5% of the time, Pallas kernels for 0%

commit v1 on v0

--- a/solution.py
+++ b/solution.py
@@ -8,6 +8,27 @@
 HEAD = 128
 QBLK = 32
 clip_ratio = 2.5
+
+
+def gather_around(shard, axis, dim):
+    length, index, rows = (lax.axis_size(axis), lax.axis_index(axis), shard.shape[dim])
+    right = [(i, (i + 1) % length) for i in range(length)]
+    backward = [(i, (i - 1) % length) for i in range(length)]
+    out = jnp.zeros((*shard.shape[:dim], length * rows, *shard.shape[dim + 1 :]), shard.dtype)
+    out = lax.dynamic_update_slice_in_dim(out, shard, index * rows, axis=dim)
+    from_left = from_right = shard
+    half = length // 2
+    for step in range(1, half + 1):
+        from_left = lax.ppermute(from_left, axis, right)
+        out = lax.dynamic_update_slice_in_dim(
+            out, from_left, (index - step) % length * rows, axis=dim
+        )
+        if step < length - half:
+            from_right = lax.ppermute(from_right, axis, backward)
+            out = lax.dynamic_update_slice_in_dim(
+                out, from_right, (index + step) % length * rows, axis=dim
+            )
+    return out
 
 
 def hadamard(length):
@@ -49,7 +70,7 @@
 def collect(pieces):
     outer_count = lax.axis_size("gx")
     inner_count = lax.axis_size("gy")
-    near_rows = lax.all_gather(pieces, "gx", axis=0, tiled=True)
+    near_rows = gather_around(pieces, "gx", 0)
     gathered = lax.all_gather(near_rows, "gy", axis=0, tiled=True)
     shaped = gathered.reshape(
         (inner_count, outer_count, gathered.shape[0] // (inner_count * outer_count))

time: 266 us -> 263 us (0.989)
  blocking collectives: 18 us -> 0 us
  waiting for transfers between devices: 139 us -> 148 us
  starting transfers between devices: 0.12 us -> 5.32 us
    all_gather x1 -> x0, blocking collectives: 18 us -> none  [collect(): near_rows = lax.all_gather(pieces, 'gx', axis=0, tiled=True)]
    ppermute x0 -> x3, waiting for transfers between devices: none -> 11 us  [the longest x2 9.65 us: gather_around(): from_left = lax.ppermute(from_left, axis, right)]
    ppermute x0 -> x3, starting transfers between devices: none -> 5.2 us  [the longest x2 3.11 us: gather_around(): from_left = lax.ppermute(from_left, axis, right)]
    unnamed x18 -> x20, local copies, waits for them, and re-layouts: 12.7 us -> 13.5 us
  transfers between devices with their start and end apart: 3 -> 6, of which waited for: 3 -> 6; matrix products, arithmetic and copies ran while one was open for 5% -> 5% of each run, Pallas kernels for 0% -> 0%
where the time goes in v1:
time: 263 us; the launch traced here: 262 us
  waiting for transfers between devices  148 us (56%)
  local copies, waits for them, and re-layouts  47.6 us (18%)
  matrix products  37.1 us (14%)
  between operations  13.9 us (5%)
  other arithmetic  9.49 us (4%)
  starting transfers between devices  5.32 us (2%)
    reduce_scatter x1, waiting for transfers between devices, body(): lax.psum_scatter(clipped(rotate(partial_value, rotation)).astype(jnp.bflo...  76.9 us
    all_gather x1, waiting for transfers between devices, collect(): gathered = lax.all_gather(near_rows, 'gy', axis=0, tiled=True)  34.4 us
    reduce_scatter x1, waiting for transfers between devices, body(): lax.psum_scatter(recoded.astype(jnp.bfloat16), 'gy', scatter_dimension=0,...  26 us
    dot_general x2, matrix products, rotate(): jnp.einsum('rhc,cd->rhd', shaped, rotation, precision=lax.Precision.HIGHEST)  16.4 us
    unnamed x20, local copies, waits for them, and re-layouts  13.5 us
    dot_general x1, local copies, waits for them, and re-layouts, rotate(): jnp.einsum('rhc,cd->rhd', shaped, rotation, precision=lax.Precision.HIGHEST)  9.9 us
    ppermute x2, waiting for transfers between devices, gather_around(): from_left = lax.ppermute(from_left, axis, right)  9.65 us
    dot_general x1, matrix products, body(): lax.dot_general(key_grad, weight, (((1,), (1,)), ((), ())), preferred_ele...  9.27 us
  transfers between devices with their start and end apart: 6, of which 6 were waited for; matrix products, arithmetic and copies ran while one was open for 5% of the time, Pallas kernels for 0%

profile of v1, /device:TPU:0, one launch (start us, length us, event | category | flops | bytes accessed | tf_op | source)
XLA Modules:
  0.0 261.9 jit_solution(16668729912864642756)
XLA Ops:
  7.2 0.0 copy-start.7
  7.2 0.0 all-gather.2.cloned.1.call-start
  7.2 0.8 mul.133
  8.1 0.9 constant_dynamic-update-slice_fusion.3
  9.0 3.1 %collective-permute-start = (bf16[128,512]{1,0:T(8,128)(2,1)S(1)}, bf16[128,512]{1,0:T(8,128)(2,1)S(1)}, u32[]{:S(2)}, u32[]{:S(2)}) collective-permute-start(bf16[128,512]{1,0:T(8,128)(2,1)S(1)} %get-tuple-element.15), channel_id=1, source_target_pairs={{0,8},{8,16},{16,24},{24,0},{1,9},{9,17},{17,25},{25,1},{2,10},{10... | collective-permute-start | bytes 393224 | tf_op jit(solution)/shard_map/ppermute | solution.py:22
  12.1 2.1 collective-permute-start.1
  14.2 4.3 %collective-permute-done = bf16[128,512]{1,0:T(8,128)(2,1)S(1)} collective-permute-done((bf16[128,512]{1,0:T(8,128)(2,1)S(1)}, bf16[128,512]{1,0:T(8,128)(2,1)S(1)}, u32[]{:S(2)}, u32[]{:S(2)}) %collective-permute-start) | collective-permute-done | bytes 131104 | tf_op jit(solution)/shard_map/ppermute | solution.py:22
  18.5 0.0 collective-permute-start.2
  18.5 1.4 collective-permute-done.1
  19.9 5.4 %collective-permute-done.2 = bf16[128,512]{1,0:T(8,128)(2,1)S(1)} collective-permute-done((bf16[128,512]{1,0:T(8,128)(2,1)S(1)}, bf16[128,512]{1,0:T(8,128)(2,1)S(1)}, u32[]{:S(2)}, u32[]{:S(2)}) %collective-permute-start.2) | collective-permute-done | bytes 131104 | tf_op jit(solution)/shard_map/ppermute | solution.py:22
  25.3 0.0 copy-start.4
  25.3 0.8 copy-done.4
  26.1 0.0 all-gather.2.cloned.1.call-update
  26.1 0.0 reduce-scatter.3.cloned.1.call-start
  26.1 1.5 copy.21
  27.7 0.0 copy-done.7
  27.7 34.4 %all-gather.2.cloned.1.call-done = bf16[4096,512]{1,0:T(8,128)(2,1)} async-done(((bf16[512,512]{1,0:T(8,128)(2,1)}), bf16[4096,512]{1,0:T(8,128)(2,1)}) %all-gather.2.cloned.1.call-update) | async-done | bytes 4194320 | tf_op jit(solution)/shard_map/all_gather | solution.py:74
  62.1 0.0 copy-start.1
  62.1 2.7 %copy.20 = bf16[4,8,128,512]{3,2,1,0:T(8,128)(2,1)S(1)} copy(bf16[4,8,128,512]{3,2,0,1:T(8,128)(2,1)} %bitcast.73) | data formatting | bytes 8388608 | tf_op jit(solution)/shard_map/transpose | solution.py:79
  64.8 0.0 copy-start
  64.8 3.2 %copy-done.1 = bf16[896,4096]{1,0:T(8,128)(2,1)S(1)} copy-done((bf16[896,4096]{1,0:T(8,128)(2,1)S(1)}, bf16[896,4096]{1,0:T(8,128)(2,1)}, u32[]{:S(2)}) %copy-start.1) | copy-done | bytes 7340056
  68.0 4.7 %multiply_reduce_fusion.1 = (f32[896,4]{0,1:T(4,128)S(1)}, f32[896,4]{0,1:T(4,128)S(1)}, f32[512,896]{1,0:T(8,128)S(1)}) fusion(f32[128]{0:T(128)S(1)} %copy-done.7, bf16[896,512]{0,1:T(8,128)(2,1)S(1)} %copy.21, bf16[4096,512]{1,0:T(8,128)(2,1)S(1)} %bitcast.71, bf16[896,4096]{1,0:T(8,128)(2,1)S(1)} %copy-done.1), kind=kOutput, calls=%fused_computation.18 | convolution fusion | flops 3760841728 | bytes 14316032 | tf_op jit(solution)/shard_map/dot_general | solution.py:84
  72.7 0.0 copy-done
  72.8 1.5 fusion.4
  74.3 0.0 copy-start.5
  74.3 0.9 copy-done.5
  75.2 6.7 %convolution_bitcast_fusion = f32[4096,512]{0,1:T(8,128)} fusion(bf16[896,512]{0,1:T(8,128)(2,1)S(1)} %get-tuple-element.16, bf16[896,4096]{1,0:T(8,128)(2,1)S(1)} %copy-done.1), kind=kOutput, calls=%fused_computation.5 | convolution fusion | flops 3758096384 | bytes 16646144 | tf_op jit(solution)/shard_map/dot_general | solution.py:92
  81.9 9.0 %copy.22 = f32[4096,512]{1,0:T(8,128)} copy(f32[4096,512]{0,1:T(8,128)} %convolution_bitcast_fusion) | data formatting | bytes 16777216 | tf_op jit(solution)/shard_map/dot_general | solution.py:92
  90.9 9.9 %dot_general.26 = f32[128,32,4,128]{3,2,1,0:T(4,128)} reshape(f32[4096,512]{1,0:T(8,128)} %copy.22) | data formatting | bytes 16777216 | tf_op jit(solution)/shard_map/rhc,cd->rhd/dot_general | solution.py:45
  100.8 16.1 %multiply_reduce_fusion = (f32[128,4]{0,1:T(4,128)S(1)}, bf16[128,32,4,128]{0,3,2,1:T(8,128)(2,1)S(1)}) fusion(f32[128,32,4,128]{3,2,1,0:T(4,128)} %dot_general.26), kind=kOutput, calls=%fused_computation.3 | convolution fusion | flops 3228106240 | bytes 12584960 | tf_op jit(solution)/shard_map/rhc,cd->rhd/dot_general | solution.py:45
  117.0 2.3 minimum_convert_fusion
  119.3 8.0 %copy.24 = bf16[128,32,4,128]{3,2,1,0:T(4,128)(2,1)} copy(bf16[128,32,4,128]{0,3,2,1:T(8,128)(2,1)} %minimum_convert_fusion) | data formatting | bytes 8388608 | tf_op jit(solution)/shard_map/convert_element_type | solution.py:96
  127.3 4.9 %copy.44 = bf16[512,8,4,128]{3,1,2,0:T(8,128)(2,1)} copy(bf16[512,8,4,128]{3,2,1,0:T(4,128)(2,1)} %bitcast.70) | data formatting | bytes 8388608
  132.2 0.0 reduce-scatter.3.cloned.1.call-update
  132.2 0.0 reduce-scatter.5.cloned.1.call-start
  132.3 76.9 %reduce-scatter.3.cloned.1.call-done = bf16[1024,512]{1,0:T(8,128)(2,1)} async-done(((bf16[4096,512]{1,0:T(8,128)(2,1)}), bf16[1024,512]{1,0:T(8,128)(2,1)}) %reduce-scatter.3.cloned.1.call-update) | async-done | bytes 1048592 | tf_op jit(solution)/shard_map/reduce_scatter | solution.py:95
  209.2 2.8 %convert_multiply_fusion = f32[1024,512]{1,0:T(8,128)} fusion(bf16[1024,512]{1,0:T(8,128)(2,1)} %reduce-scatter.3.cloned.1.call-done), kind=kLoop, calls=%fused_computation.11 | loop fusion | flops 1048576 | bytes 3145728 | tf_op jit(solution)/shard_map/mul | solution.py:51
  212.0 0.0 copy-start.2
  212.0 2.0 mul.162
  214.1 0.4 reduce_sum.43
  214.4 0.0 copy-start.3
  214.4 0.3 min.29
  214.8 0.0 copy-start.6
  214.8 0.3 max.29
  215.1 0.0 copy-done.2
  215.1 1.4 fusion.3
  216.6 0.0 reduce-scatter.5.cloned.1.call-update
  216.6 0.0 copy-done.3
  216.6 1.3 copy.27
  217.9 0.0 copy-done.6
  217.9 9.3 %convolution_convert_fusion = bf16[896,4096]{1,0:T(8,128)(2,1)} fusion(bf16[896,512]{0,1:T(8,128)(2,1)S(1)} %copy-done.6, bf16[4096,512]{1,0:T(8,128)(2,1)} %bitcast.72), kind=kOutput, calls=%fused_computation.4 | convolution fusion | flops 3761766400 | bytes 12451840 | tf_op jit(solution)/shard_map/dot_general | solution.py:88
  227.2 26.0 %reduce-scatter.5.cloned.1.call-done = bf16[128,512]{1,0:T(8,128)(2,1)} async-done(((bf16[1024,512]{1,0:T(8,128)(2,1)}), bf16[128,512]{1,0:T(8,128)(2,1)}) %reduce-scatter.5.cloned.1.call-update) | async-done | bytes 131088 | tf_op jit(solution)/shard_map/reduce_scatter | solution.py:102
  253.2 1.0 copy.25
  254.3 0.3 fusion.14
  254.6 0.8 copy.28
  (8 shorter events, 0.1 us)
Async XLA Ops:
  7.2 20.5 %copy-start.7 = (f32[128]{0:T(128)S(1)}, f32[128]{0:T(128)}, u32[]{:S(2)}) copy-start(f32[128]{0:T(128)} %param.8) | copy-start | bytes 1540
  7.2 55.0 %all-gather.2.cloned.1.call-start = ((), (), s32[]{:S(2)}) async-start(), calls=%async_computation.2 | async-start | bytes 4718592 | tf_op jit(solution)/shard_map/all_gather | solution.py:74
  9.0 9.5 %collective-permute-start = (bf16[128,512]{1,0:T(8,128)(2,1)S(1)}, bf16[128,512]{1,0:T(8,128)(2,1)S(1)}, u32[]{:S(2)}, u32[]{:S(2)}) collective-permute-start(bf16[128,512]{1,0:T(8,128)(2,1)S(1)} %get-tuple-element.15), channel_id=1, source_target_pairs={{0,8},{8,16},{16,24},{24,0},{1,9},{9,17},{17,25},{25,1},{2,10},{10... | collective-permute-start | bytes 393224 | tf_op jit(solution)/shard_map/ppermute | solution.py:22
  12.1 7.8 %collective-permute-start.1 = (bf16[128,512]{1,0:T(8,128)(2,1)S(1)}, bf16[128,512]{1,0:T(8,128)(2,1)S(1)}, u32[]{:S(2)}, u32[]{:S(2)}) collective-permute-start(bf16[128,512]{1,0:T(8,128)(2,1)S(1)} %get-tuple-element.15), channel_id=1, source_target_pairs={{0,24},{8,0},{16,8},{24,16},{1,25},{9,1},{17,9},{25,17},{2,26},{10... | collective-permute-start | bytes 393224 | tf_op jit(solution)/shard_map/ppermute | solution.py:27
  18.5 6.8 %collective-permute-start.2 = (bf16[128,512]{1,0:T(8,128)(2,1)S(1)}, bf16[128,512]{1,0:T(8,128)(2,1)S(1)}, u32[]{:S(2)}, u32[]{:S(2)}) collective-permute-start(bf16[128,512]{1,0:T(8,128)(2,1)S(1)} %collective-permute-done), channel_id=1, source_target_pairs={{0,8},{8,16},{16,24},{24,0},{1,9},{9,17},{17,25},{25,1},{2,10},{10... | collective-permute-start | bytes 393224 | tf_op jit(solution)/shard_map/ppermute | solution.py:22
  25.3 0.8 copy-start.4
  26.1 183.1 %reduce-scatter.3.cloned.1.call-start = ((), (), s32[]{:S(2)}) async-start(), calls=%async_computation.3 | async-start | bytes 5242880 | tf_op jit(solution)/shard_map/reduce_scatter | solution.py:95
  62.1 5.9 %copy-start.1 = (bf16[896,4096]{1,0:T(8,128)(2,1)S(1)}, bf16[896,4096]{1,0:T(8,128)(2,1)}, u32[]{:S(2)}) copy-start(bf16[896,4096]{1,0:T(8,128)(2,1)} %param.5) | copy-start | bytes 22020100
  64.8 7.9 %copy-start = (bf16[4,8,128,512]{3,2,1,0:T(8,128)(2,1)}, bf16[4,8,128,512]{3,2,1,0:T(8,128)(2,1)S(1)}, u32[]{:S(2)}) copy-start(bf16[4,8,128,512]{3,2,1,0:T(8,128)(2,1)S(1)} %copy.20) | copy-start | bytes 12582916
  74.3 0.9 copy-start.5
  132.2 121.0 %reduce-scatter.5.cloned.1.call-start = ((), (), s32[]{:S(2)}) async-start(), calls=%async_computation.4 | async-start | bytes 1179648 | tf_op jit(solution)/shard_map/reduce_scatter | solution.py:102
  212.0 3.1 %copy-start.2 = (bf16[1024,512]{1,0:T(8,128)(2,1)S(1)}, bf16[1024,512]{1,0:T(8,128)(2,1)}, u32[]{:S(2)}) copy-start(bf16[1024,512]{1,0:T(8,128)(2,1)} %reduce-scatter.3.cloned.1.call-done) | copy-start | bytes 3145732
  214.4 2.2 copy-start.3
  214.8 3.1 %copy-start.6 = (bf16[896,512]{0,1:T(8,128)(2,1)S(1)}, bf16[896,512]{0,1:T(8,128)(2,1)}, u32[]{:S(2)}) copy-start(bf16[896,512]{0,1:T(8,128)(2,1)} %copy-done.5) | copy-start | bytes 2752516
Sparse Core Ops, SparseCore 0:
  26.2 35.8 all-gather.1
  132.4 76.7 reduce-scatter.2
  216.7 36.4 reduce-scatter.4
